TPU v7x, 128 devices: a whole 4x4x4 slice. The times are simulated.
128 devices in a mesh: ka: 16 (over x_hi, z, core), band: 8 (over x_lo, y).
Axes of the slice: x: 4 (x_hi: 2, x_lo: 2; x = x_hi * 2 + x_lo), y: 4, z: 4, core: 2. Of those that a mesh axis runs over, the one named last changes fastest.
Arguments:
- occ_rows: bfloat16 [16, 2048, 128], P('ka', 'band'), may hold values from -0.5 to 0.5
- vir_rows: bfloat16 [16, 2048, 896], P('ka', 'band'), may hold values from -0.1875 to 0.1875
- trial_vectors: float32 [16, 2, 128, 896], P('ka', None, None, 'band'), may hold values from -6 to 6
- occ_energy: float32 [16, 128], P('ka'), may hold values from -1.2 to -0.3
- vir_energy: float32 [16, 896], P('ka', 'band'), may hold values from 0.1 to 1.5
- coulomb: bfloat16 [2048, 2048], P('band'), may hold values from -0.0625 to 0.0625
- exch_kernel: bfloat16 [16, 2048, 2048], P(None, 'band'), as said below
- minus_table: int32 [16, 16], replicated, may hold values from 0 to 15, as said below
Outputs:
- sigma_vectors: float32 [16, 2, 128, 896], P('ka', None, None, 'band')
Inputs may be any that keep to these rules, and one draw needn't show every extreme that they name: minus_table[k, q] is the k-point k - q on a group of 16 k-points: every row and every column holds each index once, and one q gives minus_table[k, q] == k for every k. Each exch_kernel[q] is symmetric.
All inputs are finite; a program needn't handle non-finite values.
Results may differ from a plain program's by a relative error of at most 0.0051.
Values may be sent and summed in bfloat16 or wider, within the bound.
A program may use at most 128 MiB of HBM per device.

v0:
```python
import jax
import jax.numpy as jnp
from jax import lax
from jax.sharding import PartitionSpec as P


def sent_to_all(array, axis):
    copies = jnp.broadcast_to(array, (lax.axis_size(axis), *array.shape))
    return lax.all_to_all(copies, axis, split_axis=0, concat_axis=0, tiled=True)


def taken_together(array, axis):
    return sent_to_all(array, axis).sum(axis=0)


def in_order(pieces, dim):
    pieces = jnp.moveaxis(pieces, 0, dim)
    dims = pieces.shape
    return pieces.reshape(*dims[:dim], dims[dim] * dims[dim + 1], *dims[dim + 2 :])


def gather_directly(array, axis, dim):
    pieces = sent_to_all(array, axis)
    return in_order(pieces, dim)


def split_up(array, dim, size):
    before, after = (array.shape[:dim], array.shape[dim + 1 :])
    return jnp.moveaxis(array.reshape(*before, size, -1, *after), dim, 0)


def summed_on_arrival(array, axis, dim):
    size = lax.axis_size(axis)
    pieces = lax.all_to_all(split_up(array, dim, size), axis, 0, 0, tiled=True)
    return jnp.sum(pieces, axis=0)


def per_device(
    occ_rows, vir_rows, trial_vectors, occ_energy, vir_energy, coulomb, exch_kernel, minus_table
):
    vectors = trial_vectors.shape[1]
    own_rows = occ_rows.shape[1]
    kpoints = lax.axis_size("ka")
    self_point = lax.axis_index("ka")
    trial_half = trial_vectors[0].astype(jnp.bfloat16)
    trial_full, vir_full = (
        lax.all_gather(trial_half, "band", axis=2, tiled=True),
        lax.all_gather(vir_rows[0], "band", axis=0, tiled=True),
    )
    auxiliary = vir_full.shape[0]
    occ_own = occ_rows[0]
    vir_own = vir_rows[0]
    mixed_rows = jnp.einsum(
        "ri,via->vra", occ_own, trial_full, preferred_element_type=jnp.float32
    ).astype(jnp.bfloat16)
    pair_block = jnp.einsum(
        "vra,na->vrn", mixed_rows, vir_full, preferred_element_type=jnp.float32
    ).astype(jnp.bfloat16)
    density_own = jnp.sum(
        mixed_rows.astype(jnp.float32) * vir_own.astype(jnp.float32)[None], axis=2
    )
    density_sum = taken_together(density_own, "ka")
    density_half = gather_directly(density_sum.astype(jnp.bfloat16), "band", 1)
    potential = jnp.einsum("vn,rn->vr", density_half, coulomb, preferred_element_type=jnp.float32)
    piece_width = auxiliary // kpoints
    kernel_cols = lax.dynamic_slice_in_dim(exch_kernel, self_point * piece_width, piece_width, 2)
    split_pairs = pair_block.reshape(vectors, own_rows, kpoints, piece_width)
    moved_pairs = jnp.take(
        lax.all_to_all(split_pairs, "ka", split_axis=2, concat_axis=2, tiled=True),
        minus_table,
        axis=2,
    )
    summed = jnp.einsum(
        "vrkqc,qrc->vrkc", moved_pairs, kernel_cols, preferred_element_type=jnp.float32
    )
    screened = lax.all_to_all(
        summed.astype(jnp.bfloat16), "ka", split_axis=2, concat_axis=2, tiled=True
    )
    screened = screened.reshape(vectors, own_rows, auxiliary)
    product = jnp.einsum("vrn,na->vra", screened, vir_full, preferred_element_type=jnp.float32)
    weights = (2.0 * potential[:, :, None] * vir_own.astype(jnp.float32)[None] - product).astype(
        jnp.bfloat16
    )
    partial_sums = jnp.einsum("ri,vra->via", occ_own, weights, preferred_element_type=jnp.float32)
    coupled = summed_on_arrival(partial_sums, "band", 2)
    energy_gaps = vir_energy[0][None, :] - occ_energy[0][:, None]
    return (energy_gaps[None] * trial_vectors[0] + coupled)[None]


def solution(mesh):
    in_specs = (
        P("ka", "band", None),
        P("ka", "band", None),
        P("ka", None, None, "band"),
        P("ka", None),
        P("ka", "band"),
        P("band", None),
        P(None, "band", None),
        P(),
    )
    out_specs = P("ka", None, None, "band")
    return jax.shard_map(
        per_device, mesh=mesh, in_specs=in_specs, out_specs=out_specs, check_vma=False
    )
```

profile of v0, /device:TPU:96, one launch (start us, length us, event | category | flops | bytes accessed | tf_op | source)
XLA Modules:
  0.0 215.4 jit_solution(1257399889311923718)
XLA Ops:
  6.5 0.7 all-gather.4.cloned.1.call-update
  7.3 1.1 bitcast_convert_fusion.1
  8.3 0.3 copy.30
  8.7 31.1 %all-gather = bf16[1,2,128,896]{2,3,1,0:T(8,128)(2,1)S(1)} all-gather(bf16[1,2,128,112]{2,3,1,0:T(8,128)(2,1)S(1)} %convert_element_type.33), channel_id=2, replica_groups=mesh['ka'=16,'band'=8] {'band'}, dimensions={3}, use_global_device_ids=true | all-gather | bytes 516096 | tf_op jit(solution)/shard_map/all_gather | solution.py:47
  39.7 0.4 multiply_reduce_fusion.1
  40.2 0.6 broadcast_in_dim.23
  40.8 6.5 %all-to-all-start = ((f32[16,2,256]{2,1,0:T(2,128)}), f32[16,2,256]{2,1,0:T(2,128)S(1)}, u32[]{:S(2)}, u32[]{:S(2)}) async-start(f32[16,2,256]{2,1,0:T(2,128)} %broadcast_in_dim.23), calls=%async_computation | async-start | bytes 65536 | tf_op jit(solution)/shard_map/all_to_all | solution.py:9
  47.3 13.7 %all-gather.4.cloned.1.call-done = bf16[1,2048,896]{2,1,0:T(8,128)(2,1)} async-done(((bf16[1,256,896]{2,1,0:T(8,128)(2,1)}), bf16[1,2048,896]{2,1,0:T(8,128)(2,1)}) %all-gather.4.cloned.1.call-update) | async-done | bytes 3670032 | tf_op jit(solution)/shard_map/all_gather | solution.py:48
  61.0 4.4 %fusion.7 = bf16[2,32,16,8,128]{4,3,2,1,0:T(8,128)(2,1)S(1)} fusion(bf16[2,256,896]{1,2,0:T(8,128)(2,1)S(1)} %get-tuple-element.6, bf16[1,2048,896]{2,1,0:T(8,128)(2,1)} %all-gather.4.cloned.1.call-done), kind=kOutput, calls=%fused_computation.11 | convolution fusion | flops 1880096768 | bytes 6684672 | tf_op jit(solution)/shard_map/vra,na->vrn/dot_general | solution.py:56
  65.5 1.9 copy.55
  67.4 6.8 %all-to-all-start.2 = ((bf16[2,256,16,128]{3,1,0,2:T(8,128)(2,1)}), bf16[2,256,16,128]{3,1,0,2:T(8,128)(2,1)S(1)}, u32[]{:S(2)}, u32[]{:S(2)}) async-start(bf16[2,256,16,128]{3,1,0,2:T(8,128)(2,1)} %bitcast.66), calls=%async_computation.2 | async-start | bytes 4194304 | tf_op jit(solution)/shard_map/all_to_all | solution.py:69
  74.2 0.1 reshape.57
  74.3 2.7 %bitcast_convert_fusion = f32[256,128,16]{1,0,2:T(8,128)} fusion(bf16[16,256,2048]{2,1,0:T(8,128)(2,1)} %param.14, s32[]{:T(128)S(6)} %select_n.12), kind=kLoop, calls=%fused_computation.16 | loop fusion | flops 524288 | bytes 3145732
  77.0 26.1 %all-to-all-done.2 = bf16[2,256,16,128]{3,1,0,2:T(8,128)(2,1)S(1)} async-done(((bf16[2,256,16,128]{3,1,0,2:T(8,128)(2,1)}), bf16[2,256,16,128]{3,1,0,2:T(8,128)(2,1)S(1)}, u32[]{:S(2)}, u32[]{:S(2)}) %all-to-all-start.2) | async-done | bytes 2097184 | tf_op jit(solution)/shard_map/all_to_all | solution.py:69
  103.1 0.6 broadcast_in_dim.24
  103.7 0.7 copy-done.1
  104.4 4.2 %all-to-all-start.1 = ((bf16[8,2,256]{2,1,0:T(2,128)(2,1)}), bf16[8,2,256]{2,1,0:T(2,128)(2,1)S(1)}, u32[]{:S(2)}, u32[]{:S(2)}) async-start(bf16[8,2,256]{2,1,0:T(2,128)(2,1)} %broadcast_in_dim.24), calls=%async_computation.1 | async-start | bytes 16384 | tf_op jit(solution)/shard_map/all_to_all | solution.py:9
  108.6 1.7 copy.34
  110.3 13.9 %gather_fusion = bf16[256,2,256,128]{3,2,1,0:T(8,128)(2,1)} fusion(bf16[2,256,16,128]{3,1,2,0:T(8,128)(2,1)S(1)} %copy.34, s32[1024]{0:T(1024)S(1)} %pad_clamp_fusion), kind=kCustom, calls=%fused_computation | custom fusion | bytes 67109888 | tf_op jit(solution)/shard_map/jit(_take)/gather | solution.py:68
  124.2 17.9 %multiply_reduce_fusion = bf16[256,128,2,16]{1,0,2,3:T(8,128)(2,1)S(1)} fusion(f32[256,128,16]{1,0,2:T(8,128)} %bitcast_convert_fusion, bf16[16,16,2,256,128]{4,3,2,1,0:T(8,128)(2,1)} %bitcast.65, pred[16,16]{1,0:T(8,128)(4,1)S(1)} %compare_and_fusion), kind=kLoop, calls=%fused_computation.1 | loop fusion | flops 66060288 | bytes 37748992
  142.1 2.6 %copy.47 = bf16[256,128,2,16]{0,1,2,3:T(8,128)(2,1)} copy(bf16[256,128,2,16]{1,0,2,3:T(8,128)(2,1)S(1)} %multiply_reduce_fusion) | data formatting | bytes 4194304 | tf_op jit(solution)/shard_map/vrkqc,qrc->vrkc/dot_general | solution.py:73
  144.7 5.5 %all-to-all-start.3 = ((bf16[2,256,16,128]{1,3,0,2:T(8,128)(2,1)}), bf16[2,256,16,128]{1,3,0,2:T(8,128)(2,1)S(1)}, u32[]{:S(2)}, u32[]{:S(2)}) async-start(bf16[2,256,16,128]{1,3,0,2:T(8,128)(2,1)} %bitcast.67), calls=%async_computation.3 | async-start | bytes 4194304 | tf_op jit(solution)/shard_map/all_to_all | solution.py:76
  150.3 0.4 convolution_multiply_fusion
  150.6 28.5 %all-to-all-done.3 = bf16[2,256,16,128]{1,3,0,2:T(8,128)(2,1)S(1)} async-done(((bf16[2,256,16,128]{1,3,0,2:T(8,128)(2,1)}), bf16[2,256,16,128]{1,3,0,2:T(8,128)(2,1)S(1)}, u32[]{:S(2)}, u32[]{:S(2)}) %all-to-all-start.3) | async-done | bytes 2097184 | tf_op jit(solution)/shard_map/all_to_all | solution.py:76
  179.2 1.5 copy.35
  180.7 5.6 %fusion.14 = f32[2,896,128]{2,1,0:T(8,128)S(1)} fusion(bf16[2,256,2048]{1,2,0:T(8,128)(2,1)} %bitcast.68, bf16[1,2048,896]{2,1,0:T(8,128)(2,1)} %all-gather.4.cloned.1.call-done, f32[2,256]{1,0:T(2,128)S(1)} %convolution_multiply_fusion, f32[256,896]{0,1:T(8,128)} %copy-done.2, bf16[1,256,128]{2,1,0:T(8,128)(2,1)S(1)} %copy-done.4), kind=kOutput, calls=%fused_computation.14 | convolution fusion | flops 1997864960 | bytes 7669760 | tf_op jit(solution)/shard_map/ri,vra->via/dot_general | solution.py:84
  186.2 0.0 copy-start.7
  186.3 1.0 copy.56
  187.2 6.6 %all-to-all-start.4 = ((f32[8,2,128,112]{2,3,1,0:T(8,128)}), f32[8,2,128,112]{2,3,1,0:T(8,128)S(1)}, u32[]{:S(2)}, u32[]{:S(2)}) async-start(f32[8,2,128,112]{2,3,1,0:T(8,128)} %bitcast.64), calls=%async_computation.4 | async-start | bytes 1835008 | tf_op jit(solution)/shard_map/all_to_all | solution.py:34
  193.9 0.1 broadcast_subtract_fusion
  194.0 13.9 %all-to-all-done.4 = f32[8,2,128,112]{2,3,1,0:T(8,128)S(1)} async-done(((f32[8,2,128,112]{2,3,1,0:T(8,128)}), f32[8,2,128,112]{2,3,1,0:T(8,128)S(1)}, u32[]{:S(2)}, u32[]{:S(2)}) %all-to-all-start.4) | async-done | bytes 917536 | tf_op jit(solution)/shard_map/all_to_all | solution.py:34
  207.9 0.7 bitcast_add_fusion
  (23 shorter events, 0.1 us)
Async XLA Ops:
  6.5 143.7 %copy-start = (bf16[256,2048]{1,0:T(8,128)(2,1)S(1)}, bf16[256,2048]{1,0:T(8,128)(2,1)}, u32[]{:S(2)}) copy-start(bf16[256,2048]{1,0:T(8,128)(2,1)} %param.13) | copy-start | bytes 3145732
  6.5 2.1 copy-start.3
  6.5 33.2 %copy-start.4 = (bf16[1,256,128]{2,1,0:T(8,128)(2,1)S(1)}, bf16[1,256,128]{2,1,0:T(8,128)(2,1)}, u32[]{:S(2)}) copy-start(bf16[1,256,128]{2,1,0:T(8,128)(2,1)} %param.8) | copy-start | bytes 196612
  6.5 54.5 %all-gather.4.cloned.1.call-start = ((), (), s32[]{:S(2)}) async-start(), calls=%async_computation.5 | async-start | bytes 4128768 | tf_op jit(solution)/shard_map/all_gather | solution.py:48
  8.7 56.8 %copy-start.2 = (f32[256,896]{0,1:T(8,128)}, f32[256,896]{0,1:T(8,128)S(1)}, u32[]{:S(2)}) copy-start(f32[256,896]{0,1:T(8,128)S(1)} %copy.30) | copy-start | bytes 2752516
  40.8 26.6 %all-to-all-start = ((f32[16,2,256]{2,1,0:T(2,128)}), f32[16,2,256]{2,1,0:T(2,128)S(1)}, u32[]{:S(2)}, u32[]{:S(2)}) async-start(f32[16,2,256]{2,1,0:T(2,128)} %broadcast_in_dim.23), calls=%async_computation | async-start | bytes 65536 | tf_op jit(solution)/shard_map/all_to_all | solution.py:9
  67.4 6.8 %copy-start.5 = (s32[16,16]{1,0:T(8,128)S(1)}, s32[16,16]{1,0:T(8,128)}, u32[]{:S(2)}) copy-start(s32[16,16]{1,0:T(8,128)} %param.15) | copy-start | bytes 3076
  67.4 35.7 %all-to-all-start.2 = ((bf16[2,256,16,128]{3,1,0,2:T(8,128)(2,1)}), bf16[2,256,16,128]{3,1,0,2:T(8,128)(2,1)S(1)}, u32[]{:S(2)}, u32[]{:S(2)}) async-start(bf16[2,256,16,128]{3,1,0,2:T(8,128)(2,1)} %bitcast.66), calls=%async_computation.2 | async-start | bytes 4194304 | tf_op jit(solution)/shard_map/all_to_all | solution.py:69
  103.1 1.3 copy-start.1
  104.4 40.3 %all-to-all-start.1 = ((bf16[8,2,256]{2,1,0:T(2,128)(2,1)}), bf16[8,2,256]{2,1,0:T(2,128)(2,1)S(1)}, u32[]{:S(2)}, u32[]{:S(2)}) async-start(bf16[8,2,256]{2,1,0:T(2,128)(2,1)} %broadcast_in_dim.24), calls=%async_computation.1 | async-start | bytes 16384 | tf_op jit(solution)/shard_map/all_to_all | solution.py:9
  144.7 34.5 %all-to-all-start.3 = ((bf16[2,256,16,128]{1,3,0,2:T(8,128)(2,1)}), bf16[2,256,16,128]{1,3,0,2:T(8,128)(2,1)S(1)}, u32[]{:S(2)}, u32[]{:S(2)}) async-start(bf16[2,256,16,128]{1,3,0,2:T(8,128)(2,1)} %bitcast.67), calls=%async_computation.3 | async-start | bytes 4194304 | tf_op jit(solution)/shard_map/all_to_all | solution.py:76
  186.2 7.6 %copy-start.6 = (f32[1,128]{1,0:T(1,128)S(1)}, f32[1,128]{1,0:T(1,128)}, u32[]{:S(2)}) copy-start(f32[1,128]{1,0:T(1,128)} %param.11) | copy-start | bytes 1540
  186.2 7.6 %copy-start.7 = (f32[1,112]{1,0:T(1,128)S(1)}, f32[1,112]{1,0:T(1,128)}, u32[]{:S(2)}) copy-start(f32[1,112]{1,0:T(1,128)} %param.12) | copy-start | bytes 1348
  187.2 20.6 %all-to-all-start.4 = ((f32[8,2,128,112]{2,3,1,0:T(8,128)}), f32[8,2,128,112]{2,3,1,0:T(8,128)S(1)}, u32[]{:S(2)}, u32[]{:S(2)}) async-start(f32[8,2,128,112]{2,3,1,0:T(8,128)} %bitcast.64), calls=%async_computation.4 | async-start | bytes 1835008 | tf_op jit(solution)/shard_map/all_to_all | solution.py:34
Sparse Core Ops, SparseCore 0:
  9.0 52.0 all-gather.3
where the time goes:
time: 216 us; the launch traced here: 215 us
  waiting for transfers between devices  82.9 us (38%)
  blocking collectives  31.1 us (14%)
  starting transfers between devices  29.6 us (14%)
  local copies, waits for them, and re-layouts  25 us (12%)
  other arithmetic  22.5 us (10%)
  between operations  13.5 us (6%)
  matrix products  10.8 us (5%)
    all_gather x1, blocking collectives, per_device(): lax.all_gather(trial_half, 'band', axis=2, tiled=True)  31.1 us
    all_to_all x1, waiting for transfers between devices, per_device(): lax.all_to_all(summed.astype(jnp.bfloat16), 'ka', split_axis=2, concat_ax...  28.5 us
    all_to_all x1, waiting for transfers between devices, per_device(): lax.all_to_all(split_pairs, 'ka', split_axis=2, concat_axis=2, tiled=True)  26.1 us
    unnamed x2, other arithmetic  20.6 us
    gather x1, local copies, waits for them, and re-layouts, per_device(): jnp.take(lax.all_to_all(split_pairs, 'ka', split_axis=2, concat_axis=2, t...  13.9 us
    all_to_all x1, waiting for transfers between devices, summed_on_arrival(): pieces = lax.all_to_all(split_up(array, dim, size), axis, 0, 0, tiled=True)  13.9 us
    all_gather x1, waiting for transfers between devices, per_device(): lax.all_gather(vir_rows[0], 'band', axis=0, tiled=True)  13.7 us
    all_to_all x2, starting transfers between devices, sent_to_all(): return lax.all_to_all(copies, axis, split_axis=0, concat_axis=0, tiled=True)  10.7 us
  transfers between devices with their start and end apart: 6, of which 4 were waited for; matrix products, arithmetic and copies ran while one was open for 22% of the time, Pallas kernels for 0%

commit v1 on v0

--- a/solution.py
+++ b/solution.py
@@ -66,7 +66,12 @@
     kernel_cols = lax.dynamic_slice_in_dim(exch_kernel, self_point * piece_width, piece_width, 2)
     split_pairs = pair_block.reshape(vectors, own_rows, kpoints, piece_width)
     moved_pairs = jnp.take(
-        lax.all_to_all(split_pairs, "ka", split_axis=2, concat_axis=2, tiled=True),
+        jnp.concatenate(
+            lax.all_to_all(
+                jnp.stack(jnp.split(split_pairs, lax.axis_size("ka"), axis=2)), "ka", 0, 0
+            ),
+            axis=2,
+        ),
         minus_table,
         axis=2,
     )

time: 216 us -> 219 us (1.014)
  local copies, waits for them, and re-layouts: 25 us -> 27.8 us
    split x0 -> x1, local copies, waits for them, and re-layouts: none -> 4.8 us  [per_device(): jnp.split(split_pairs, lax.axis_size('ka'), axis=2)]
  transfers between devices with their start and end apart: 6 -> 6, of which waited for: 4 -> 4; matrix products, arithmetic and copies ran while one was open for 22% -> 23% of each run, Pallas kernels for 0% -> 0%
where the time goes in v1:
time: 219 us; the launch traced here: 218 us
  waiting for transfers between devices  82.9 us (38%)
  blocking collectives  31.1 us (14%)
  starting transfers between devices  29.6 us (14%)
  local copies, waits for them, and re-layouts  27.8 us (13%)
  other arithmetic  22.5 us (10%)
  between operations  13.7 us (6%)
  matrix products  10.8 us (5%)
    all_gather x1, blocking collectives, per_device(): lax.all_gather(trial_half, 'band', axis=2, tiled=True)  31.1 us
    all_to_all x1, waiting for transfers between devices, per_device(): lax.all_to_all(summed.astype(jnp.bfloat16), 'ka', split_axis=2, concat_ax...  28.5 us
    all_to_all x1, waiting for transfers between devices, per_device(): lax.all_to_all(jnp.stack(jnp.split(split_pairs, lax.axis_size('ka'), axis...  26 us
    unnamed x2, other arithmetic  20.6 us
    gather x1, local copies, waits for them, and re-layouts, per_device(): jnp.take(jnp.concatenate(lax.all_to_all(jnp.stack(jnp.split(split_pairs,...  13.9 us
    all_to_all x1, waiting for transfers between devices, summed_on_arrival(): pieces = lax.all_to_all(split_up(array, dim, size), axis, 0, 0, tiled=True)  13.9 us
    all_gather x1, waiting for transfers between devices, per_device(): lax.all_gather(vir_rows[0], 'band', axis=0, tiled=True)  13.7 us
    all_to_all x2, starting transfers between devices, sent_to_all(): return lax.all_to_all(copies, axis, split_axis=0, concat_axis=0, tiled=True)  10.7 us
  transfers between devices with their start and end apart: 6, of which 4 were waited for; matrix products, arithmetic and copies ran while one was open for 23% of the time, Pallas kernels for 0%

profile of v1, /device:TPU:96, one launch (start us, length us, event | category | flops | bytes accessed | tf_op | source)
XLA Modules:
  0.0 218.3 jit_solution(15779257758847403715)
XLA Ops:
  6.5 0.7 all-gather.4.cloned.1.call-update
  7.3 1.1 bitcast_convert_fusion.1
  8.3 0.3 copy.88
  8.7 31.1 %all-gather = bf16[1,2,128,896]{2,3,1,0:T(8,128)(2,1)S(1)} all-gather(bf16[1,2,128,112]{2,3,1,0:T(8,128)(2,1)S(1)} %convert_element_type.33), channel_id=2, replica_groups=mesh['ka'=16,'band'=8] {'band'}, dimensions={3}, use_global_device_ids=true | all-gather | bytes 516096 | tf_op jit(solution)/shard_map/all_gather | solution.py:47
  39.7 0.4 multiply_reduce_fusion.1
  40.2 0.6 broadcast_in_dim.23
  40.8 6.5 %all-to-all-start = ((f32[16,2,256]{2,1,0:T(2,128)}), f32[16,2,256]{2,1,0:T(2,128)S(1)}, u32[]{:S(2)}, u32[]{:S(2)}) async-start(f32[16,2,256]{2,1,0:T(2,128)} %broadcast_in_dim.23), calls=%async_computation | async-start | bytes 65536 | tf_op jit(solution)/shard_map/all_to_all | solution.py:9
  47.3 13.7 %all-gather.4.cloned.1.call-done = bf16[1,2048,896]{2,1,0:T(8,128)(2,1)} async-done(((bf16[1,256,896]{2,1,0:T(8,128)(2,1)}), bf16[1,2048,896]{2,1,0:T(8,128)(2,1)}) %all-gather.4.cloned.1.call-update) | async-done | bytes 3670032 | tf_op jit(solution)/shard_map/all_gather | solution.py:48
  61.0 4.4 %fusion.4 = bf16[2,256,2048]{2,1,0:T(8,128)(2,1)S(1)} fusion(bf16[2,256,896]{1,2,0:T(8,128)(2,1)S(1)} %get-tuple-element.22, bf16[1,2048,896]{2,1,0:T(8,128)(2,1)} %all-gather.4.cloned.1.call-done), kind=kOutput, calls=%fused_computation.6 | convolution fusion | flops 1880096768 | bytes 6684672 | tf_op jit(solution)/shard_map/vra,na->vrn/dot_general | solution.py:56
  65.5 0.6 copy.140
  66.1 4.8 %fusion.34 = (bf16[2,256,1,128]{3,2,1,0:T(2,128)(2,1)S(1)}, bf16[2,256,1,128]{3,2,1,0:T(2,128)(2,1)S(1)}, bf16[2,256,1,128]{3,2,1,0:T(2,128)(2,1)S(1)}, bf16[2,2...) fusion(bf16[2,256,16,128]{3,2,1,0:T(8,128)(2,1)S(1)} %bitcast.131), kind=kLoop, calls=%fused_computation.59 | loop fusion | bytes 4194304 | tf_op jit(solution)/shard_map/split | solution.py:71
  71.5 1.3 copy-done.2
  72.8 6.8 %all-to-all-start.2 = ((bf16[16,2,256,1,128]{4,2,1,3,0:T(8,128)(2,1)}), bf16[16,2,256,1,128]{4,2,1,3,0:T(8,128)(2,1)S(1)}, u32[]{:S(2)}, u32[]{:S(2)}) async-start(bf16[16,2,256,1,128]{4,2,1,3,0:T(8,128)(2,1)} %copy-done.2), calls=%async_computation.2 | async-start | bytes 4194304 | tf_op jit(solution)/shard_map/all_to_all | solution.py:70
  79.6 0.1 reshape.65
  79.7 2.7 %bitcast_convert_fusion = f32[256,128,16]{1,0,2:T(8,128)} fusion(bf16[16,256,2048]{2,1,0:T(8,128)(2,1)} %param.14, s32[]{:T(128)S(6)} %select_n.12), kind=kLoop, calls=%fused_computation.14 | loop fusion | flops 524288 | bytes 3145732
  82.5 26.0 %all-to-all-done.2 = bf16[16,2,256,1,128]{4,2,1,3,0:T(8,128)(2,1)S(1)} async-done(((bf16[16,2,256,1,128]{4,2,1,3,0:T(8,128)(2,1)}), bf16[16,2,256,1,128]{4,2,1,3,0:T(8,128)(2,1)S(1)}, u32[]{:S(2)}, u32[]{:S(2)}) %all-to-all-start.2) | async-done | bytes 2097184 | tf_op jit(solution)/shard_map/all_to_all | solution.py:70
  108.5 0.6 broadcast_in_dim.24
  109.1 4.2 %all-to-all-start.1 = ((bf16[8,2,256]{2,1,0:T(2,128)(2,1)}), bf16[8,2,256]{2,1,0:T(2,128)(2,1)S(1)}, u32[]{:S(2)}, u32[]{:S(2)}) async-start(bf16[8,2,256]{2,1,0:T(2,128)(2,1)} %broadcast_in_dim.24), calls=%async_computation.1 | async-start | bytes 16384 | tf_op jit(solution)/shard_map/all_to_all | solution.py:9
  113.3 13.9 %gather_fusion = bf16[256,2,256,128]{3,2,1,0:T(8,128)(2,1)} fusion(bf16[2,256,16,128]{3,1,0,2:T(8,128)(2,1)S(1)} %bitcast.129, s32[1024]{0:T(1024)S(1)} %pad_clamp_fusion), kind=kCustom, calls=%fused_computation | custom fusion | bytes 67109888 | tf_op jit(solution)/shard_map/jit(_take)/gather | solution.py:68
  127.2 17.9 %multiply_reduce_fusion = bf16[256,128,2,16]{1,0,2,3:T(8,128)(2,1)S(1)} fusion(f32[256,128,16]{1,0,2:T(8,128)} %bitcast_convert_fusion, bf16[16,16,2,256,128]{4,3,2,1,0:T(8,128)(2,1)} %bitcast.130, pred[16,16]{1,0:T(8,128)(4,1)S(1)} %compare_and_fusion), kind=kLoop, calls=%fused_computation.1 | loop fusion | flops 66060288 | bytes 37748992
  145.1 2.6 %copy.119 = bf16[256,128,2,16]{0,1,2,3:T(8,128)(2,1)} copy(bf16[256,128,2,16]{1,0,2,3:T(8,128)(2,1)S(1)} %multiply_reduce_fusion) | data formatting | bytes 4194304 | tf_op jit(solution)/shard_map/vrkqc,qrc->vrkc/dot_general | solution.py:78
  147.7 5.5 %all-to-all-start.3 = ((bf16[2,256,16,128]{1,3,0,2:T(8,128)(2,1)}), bf16[2,256,16,128]{1,3,0,2:T(8,128)(2,1)S(1)}, u32[]{:S(2)}, u32[]{:S(2)}) async-start(bf16[2,256,16,128]{1,3,0,2:T(8,128)(2,1)} %bitcast.132), calls=%async_computation.3 | async-start | bytes 4194304 | tf_op jit(solution)/shard_map/all_to_all | solution.py:81
  153.2 0.4 convolution_multiply_fusion
  153.6 28.5 %all-to-all-done.3 = bf16[2,256,16,128]{1,3,0,2:T(8,128)(2,1)S(1)} async-done(((bf16[2,256,16,128]{1,3,0,2:T(8,128)(2,1)}), bf16[2,256,16,128]{1,3,0,2:T(8,128)(2,1)S(1)}, u32[]{:S(2)}, u32[]{:S(2)}) %all-to-all-start.3) | async-done | bytes 2097184 | tf_op jit(solution)/shard_map/all_to_all | solution.py:81
  182.2 1.5 copy.107
  183.6 5.6 %fusion.11 = f32[2,896,128]{2,1,0:T(8,128)S(1)} fusion(bf16[2,256,2048]{1,2,0:T(8,128)(2,1)} %bitcast.133, bf16[1,2048,896]{2,1,0:T(8,128)(2,1)} %all-gather.4.cloned.1.call-done, f32[2,256]{1,0:T(2,128)S(1)} %convolution_multiply_fusion, f32[256,896]{0,1:T(8,128)} %copy-done.1, bf16[1,256,128]{2,1,0:T(8,128)(2,1)S(1)} %copy-done.4), kind=kOutput, calls=%fused_computation.12 | convolution fusion | flops 1997864960 | bytes 7669760 | tf_op jit(solution)/shard_map/ri,vra->via/dot_general | solution.py:89
  189.2 0.0 copy-start.7
  189.2 1.0 copy.190
  190.2 6.6 %all-to-all-start.4 = ((f32[8,2,128,112]{2,3,1,0:T(8,128)}), f32[8,2,128,112]{2,3,1,0:T(8,128)S(1)}, u32[]{:S(2)}, u32[]{:S(2)}) async-start(f32[8,2,128,112]{2,3,1,0:T(8,128)} %bitcast.128), calls=%async_computation.4 | async-start | bytes 1835008 | tf_op jit(solution)/shard_map/all_to_all | solution.py:34
  196.8 0.1 broadcast_subtract_fusion
  196.9 13.9 %all-to-all-done.4 = f32[8,2,128,112]{2,3,1,0:T(8,128)S(1)} async-done(((f32[8,2,128,112]{2,3,1,0:T(8,128)}), f32[8,2,128,112]{2,3,1,0:T(8,128)S(1)}, u32[]{:S(2)}, u32[]{:S(2)}) %all-to-all-start.4) | async-done | bytes 917536 | tf_op jit(solution)/shard_map/all_to_all | solution.py:34
  210.8 0.7 bitcast_add_fusion
  (39 shorter events, 0.6 us)
Async XLA Ops:
  6.5 146.7 %copy-start = (bf16[256,2048]{1,0:T(8,128)(2,1)S(1)}, bf16[256,2048]{1,0:T(8,128)(2,1)}, u32[]{:S(2)}) copy-start(bf16[256,2048]{1,0:T(8,128)(2,1)} %param.13) | copy-start | bytes 3145732
  6.5 2.1 copy-start.3
  6.5 33.2 %copy-start.4 = (bf16[1,256,128]{2,1,0:T(8,128)(2,1)S(1)}, bf16[1,256,128]{2,1,0:T(8,128)(2,1)}, u32[]{:S(2)}) copy-start(bf16[1,256,128]{2,1,0:T(8,128)(2,1)} %param.8) | copy-start | bytes 196612
  6.5 54.5 %all-gather.4.cloned.1.call-start = ((), (), s32[]{:S(2)}) async-start(), calls=%async_computation.5 | async-start | bytes 4128768 | tf_op jit(solution)/shard_map/all_gather | solution.py:48
  8.7 56.8 %copy-start.1 = (f32[256,896]{0,1:T(8,128)}, f32[256,896]{0,1:T(8,128)S(1)}, u32[]{:S(2)}) copy-start(f32[256,896]{0,1:T(8,128)S(1)} %copy.88) | copy-start | bytes 2752516
  40.8 32.0 %all-to-all-start = ((f32[16,2,256]{2,1,0:T(2,128)}), f32[16,2,256]{2,1,0:T(2,128)S(1)}, u32[]{:S(2)}, u32[]{:S(2)}) async-start(f32[16,2,256]{2,1,0:T(2,128)} %broadcast_in_dim.23), calls=%async_computation | async-start | bytes 65536 | tf_op jit(solution)/shard_map/all_to_all | solution.py:9
  71.5 1.3 copy-start.2
  72.8 6.8 %copy-start.5 = (s32[16,16]{1,0:T(8,128)S(1)}, s32[16,16]{1,0:T(8,128)}, u32[]{:S(2)}) copy-start(s32[16,16]{1,0:T(8,128)} %param.15) | copy-start | bytes 3076
  72.8 35.7 %all-to-all-start.2 = ((bf16[16,2,256,1,128]{4,2,1,3,0:T(8,128)(2,1)}), bf16[16,2,256,1,128]{4,2,1,3,0:T(8,128)(2,1)S(1)}, u32[]{:S(2)}, u32[]{:S(2)}) async-start(bf16[16,2,256,1,128]{4,2,1,3,0:T(8,128)(2,1)} %copy-done.2), calls=%async_computation.2 | async-start | bytes 4194304 | tf_op jit(solution)/shard_map/all_to_all | solution.py:70
  109.1 38.6 %all-to-all-start.1 = ((bf16[8,2,256]{2,1,0:T(2,128)(2,1)}), bf16[8,2,256]{2,1,0:T(2,128)(2,1)S(1)}, u32[]{:S(2)}, u32[]{:S(2)}) async-start(bf16[8,2,256]{2,1,0:T(2,128)(2,1)} %broadcast_in_dim.24), calls=%async_computation.1 | async-start | bytes 16384 | tf_op jit(solution)/shard_map/all_to_all | solution.py:9
  147.7 34.5 %all-to-all-start.3 = ((bf16[2,256,16,128]{1,3,0,2:T(8,128)(2,1)}), bf16[2,256,16,128]{1,3,0,2:T(8,128)(2,1)S(1)}, u32[]{:S(2)}, u32[]{:S(2)}) async-start(bf16[2,256,16,128]{1,3,0,2:T(8,128)(2,1)} %bitcast.132), calls=%async_computation.3 | async-start | bytes 4194304 | tf_op jit(solution)/shard_map/all_to_all | solution.py:81
  189.2 7.6 %copy-start.6 = (f32[1,128]{1,0:T(1,128)S(1)}, f32[1,128]{1,0:T(1,128)}, u32[]{:S(2)}) copy-start(f32[1,128]{1,0:T(1,128)} %param.11) | copy-start | bytes 1540
  189.2 7.6 %copy-start.7 = (f32[1,112]{1,0:T(1,128)S(1)}, f32[1,112]{1,0:T(1,128)}, u32[]{:S(2)}) copy-start(f32[1,112]{1,0:T(1,128)} %param.12) | copy-start | bytes 1348
  190.2 20.6 %all-to-all-start.4 = ((f32[8,2,128,112]{2,3,1,0:T(8,128)}), f32[8,2,128,112]{2,3,1,0:T(8,128)S(1)}, u32[]{:S(2)}, u32[]{:S(2)}) async-start(f32[8,2,128,112]{2,3,1,0:T(8,128)} %bitcast.128), calls=%async_computation.4 | async-start | bytes 1835008 | tf_op jit(solution)/shard_map/all_to_all | solution.py:34
Sparse Core Ops, SparseCore 0:
  9.0 52.0 all-gather.3
